TPU v7x, 32 devices: a whole 2x2x4 slice. The times are simulated.
32 devices in a mesh: dp: 4 (over y, x), samp: 4 (over z), col: 2 (over core).
Axes of the slice: x: 2, y: 2, z: 4, core: 2. Of those that a mesh axis runs over, the one named last changes fastest.
Arguments:
- looked_rows: bfloat16 [16, 1920, 128], P(('dp', 'samp'), None, 'col'), may hold values from -6 to 6
- bag_ids: int32 [16, 1920], P(('dp', 'samp')), may hold values from 0 to 959, never falling along the last dimension, each value on 1 to 4 neighbouring positions
- slot_of: int32 [40], replicated, may hold values from 0 to 39, each once
- labels: int32 [384], P(('dp', 'samp')), may hold values 0 or 1
- out_weight: bfloat16 [3, 128], replicated, may hold values from -0.02734375 to 0.02734375
- filter_first: bfloat16 [128, 1521], replicated, may hold values from -0.15625 to 0.15625
- filter_second: bfloat16 [128, 4992], replicated, may hold values from -0.078125 to 0.078125
- filter_third: bfloat16 [128, 4992], replicated, may hold values from -0.078125 to 0.078125
Outputs:
- row_grads: bfloat16 [16, 1920, 128], P(('dp', 'samp'), None, 'col')
- grad_first: float32 [128, 1521], P('dp')
- grad_second: float32 [128, 4992], P('dp')
- grad_third: float32 [128, 4992], P('dp')
Inputs may be any that keep to these rules, and one draw needn't show every extreme that they name: `bag_ids`: within each owner's row, bag numbers never fall; each of the 960 bags has 1 to 4 entries and some bag exactly 4. `slot_of`: each slot number once.
All inputs are finite; a program needn't handle non-finite values. No bound on the sum of `labels` on one device may be relied on, other than what follows from the above.
Results may differ from a plain program's by a relative error of at most 0.014.
Values may be sent and summed in bfloat16 or wider, within the bound.
No kernel may reach another device: no remote copies, remote signals or barrier semaphores. Data moves between devices by JAX's collectives and lax.ppermute only.
A program may use at most 64 MiB of HBM per device.

v0:
```python
import jax
import jax.numpy as jnp
from jax import lax
from jax.sharding import PartitionSpec as P

FIELDS = 39
loss_scale = 16.0
block_rows = 4


def outer_block(previous, anchor):
    spread_rows = previous.astype(jnp.float32)[:, None, :] * anchor.astype(jnp.float32)[None, :, :]
    return spread_rows.astype(jnp.bfloat16)


def forward_layer(filter_cube, previous, anchor):

    def one_block(operands):
        outer_products = outer_block(operands[0], operands[1])
        projected_maps = jnp.einsum(
            "ocf,cfl->ol", filter_cube, outer_products, preferred_element_type=jnp.float32
        )
        return projected_maps.astype(jnp.bfloat16)

    return lax.map(one_block, (previous, anchor))


def backward_layer(filter_cube, cotangent, previous, anchor):

    def accumulate(running, operands):
        cotangent_part, previous_block, anchor_block = operands
        outer_products = outer_block(previous_block, anchor_block)
        running = running + jnp.einsum(
            "ol,cfl->ocf", cotangent_part, outer_products, preferred_element_type=jnp.float32
        )
        spread_rows = jnp.einsum(
            "ocf,ol->cfl", filter_cube, cotangent_part, preferred_element_type=jnp.float32
        )
        grad_previous = jnp.sum(spread_rows * anchor_block.astype(jnp.float32)[None, :, :], axis=1)
        grad_anchor = jnp.sum(spread_rows * previous_block.astype(jnp.float32)[:, None, :], axis=0)
        return (running, (grad_previous, grad_anchor))

    starting = jnp.zeros(filter_cube.shape, jnp.float32)
    running, (grad_previous, grad_anchor) = lax.scan(
        accumulate, starting, (cotangent, previous, anchor)
    )
    return (
        running.reshape(filter_cube.shape[0], filter_cube.shape[1] * filter_cube.shape[2]),
        grad_previous,
        grad_anchor,
    )


def local(
    looked_rows, bag_ids, slot_of, labels, out_weight, filter_first, filter_second, filter_third
):
    samples = labels.shape[0]
    slots = slot_of.shape[0]
    bag_count = samples * slots
    owners = lax.axis_size("samp")
    group_size = samples * owners
    slot_span = slots // owners
    blocks = samples // block_rows
    entries = bag_ids[0]
    member = (entries[None, :] == jnp.arange(bag_count, dtype=jnp.int32)[:, None]).astype(
        jnp.bfloat16
    )
    pooled = jnp.dot(member, looked_rows[0], preferred_element_type=jnp.float32).astype(
        jnp.bfloat16
    )
    width = pooled.shape[1]
    lanes = block_rows * width
    pooled = pooled.reshape(group_size, slot_span, width)
    arrived = lax.all_to_all(pooled, "samp", split_axis=0, concat_axis=1, tiled=True)
    chooser = (slot_of[:FIELDS][:, None] == jnp.arange(slots, dtype=jnp.int32)[None, :]).astype(
        jnp.bfloat16
    )
    arrived_blocks = arrived.reshape(blocks, block_rows, slots, width)
    anchor = jnp.einsum(
        "fk,nbkd->nfbd", chooser, arrived_blocks, preferred_element_type=jnp.float32
    ).astype(jnp.bfloat16)
    anchor = anchor.reshape(blocks, FIELDS, lanes)
    cube_first = filter_first.reshape(filter_first.shape[0], FIELDS, FIELDS)
    cube_second = filter_second.reshape(
        filter_second.shape[0], filter_second.shape[1] // FIELDS, FIELDS
    )
    cube_third = filter_third.reshape(
        filter_third.shape[0], filter_third.shape[1] // FIELDS, FIELDS
    )
    maps_count = filter_first.shape[0]
    layer_one = forward_layer(cube_first, anchor, anchor)
    layer_two = forward_layer(cube_second, layer_one, anchor)
    layer_three = forward_layer(cube_third, layer_two, anchor)

    def column_sums(layer):
        summed = jnp.sum(
            layer.astype(jnp.float32).reshape(blocks, maps_count, block_rows, width), axis=3
        )
        return summed.transpose(0, 2, 1).reshape(samples, maps_count)

    maps_one, maps_two, maps_three = lax.psum(
        (column_sums(layer_one), column_sums(layer_two), column_sums(layer_three)), "col"
    )
    weights_out = out_weight.astype(jnp.float32)
    logits = jnp.dot(maps_one, weights_out[0], precision=lax.Precision.HIGHEST)
    logits = logits + jnp.dot(maps_two, weights_out[1], precision=lax.Precision.HIGHEST)
    logits = logits + jnp.dot(maps_three, weights_out[2], precision=lax.Precision.HIGHEST)
    residual_slope = loss_scale * (jax.nn.sigmoid(logits) - labels.astype(jnp.float32))

    def direct_term(weight_row):
        scaled = (residual_slope[:, None] * weight_row[None, :]).reshape(
            blocks, block_rows, maps_count
        )
        scaled = scaled.transpose(0, 2, 1)[:, :, :, None]
        return jnp.broadcast_to(scaled, (blocks, maps_count, block_rows, width)).reshape(
            blocks, maps_count, lanes
        )

    cotan_three = direct_term(weights_out[2]).astype(jnp.bfloat16)
    grad_three, back_two, base_three = backward_layer(cube_third, cotan_three, layer_two, anchor)
    cotan_two = (direct_term(weights_out[1]) + back_two).astype(jnp.bfloat16)
    grad_two, back_one, base_two = backward_layer(cube_second, cotan_two, layer_one, anchor)
    cotan_one = (direct_term(weights_out[0]) + back_one).astype(jnp.bfloat16)
    grad_one, back_zero, base_one = backward_layer(cube_first, cotan_one, anchor, anchor)
    grad_fields = (back_zero + base_one + base_two + base_three).astype(jnp.bfloat16)
    grad_fields = grad_fields.reshape(blocks, FIELDS, block_rows, width)
    slot_grads = jnp.einsum(
        "fk,nfbd->nbkd", chooser, grad_fields, preferred_element_type=jnp.float32
    ).astype(jnp.bfloat16)
    slot_grads = slot_grads.reshape(samples, slots, width)
    returned = lax.all_to_all(slot_grads, "samp", split_axis=1, concat_axis=0, tiled=True)
    bag_grads = returned.reshape(bag_count, width)
    row_grads = jnp.einsum(
        "be,bd->ed", member, bag_grads, preferred_element_type=jnp.float32
    ).astype(jnp.bfloat16)
    shares = (
        lax.psum_scatter(
            grad_one.astype(jnp.bfloat16), "dp", scatter_dimension=0, tiled=True
        ).astype(jnp.float32),
        lax.psum_scatter(
            grad_two.astype(jnp.bfloat16), "dp", scatter_dimension=0, tiled=True
        ).astype(jnp.float32),
        lax.psum_scatter(
            grad_three.astype(jnp.bfloat16), "dp", scatter_dimension=0, tiled=True
        ).astype(jnp.float32),
    )
    summed = (
        lax.psum(shares[0].astype(jnp.bfloat16), ("samp", "col")).astype(jnp.float32),
        lax.psum(shares[1].astype(jnp.bfloat16), ("samp", "col")).astype(jnp.float32),
        lax.psum(shares[2].astype(jnp.bfloat16), ("samp", "col")).astype(jnp.float32),
    )
    return (row_grads[None], summed[0], summed[1], summed[2])


def solution(mesh):
    in_specs = (
        P(("dp", "samp"), None, "col"),
        P(("dp", "samp"), None),
        P(),
        P(("dp", "samp")),
        P(),
        P(),
        P(),
        P(),
    )
    out_specs = (P(("dp", "samp"), None, "col"), P("dp", None), P("dp", None), P("dp", None))
    return jax.shard_map(local, mesh=mesh, in_specs=in_specs, out_specs=out_specs, check_vma=False)
```

profile of v0, /device:TPU:0, one launch (start us, length us, event | category | flops | bytes accessed | tf_op | source)
XLA Modules:
  0.0 423.8 jit_solution(5831816907563971014)
XLA Ops:
  10.8 6.3 %all-to-all-start = ((bf16[4,2,7680]{2,1,0:T(2,128)(2,1)}), bf16[4,2,7680]{2,1,0:T(2,128)(2,1)S(1)}, u32[]{:S(2)}, u32[]{:S(2)}) async-start(bf16[4,2,7680]{2,1,0:T(2,128)(2,1)} %reshape.218), calls=%async_computation | async-start | bytes 245760 | tf_op jit(solution)/shard_map/all_to_all | solution.py:74
  32.3 9.0 %while.75 = (s32[]{:T(128)}, bf16[6,128,256]{1,2,0:T(8,128)(2,1)S(1)}, bf16[6,39,256]{2,1,0:T(8,128)(2,1)S(1)}, bf16[128,39,39]{0,2,1:T(8,128)(2,1)}, s32[]{:T(128)}) while((s32[]{:T(128)}, bf16[6,128,256]{1,2,0:T(8,128)(2,1)S(1)}, bf16[6,39,256]{2,1,0:T(8,128)(2,1)S(1)}, bf16[128,39,39]{0,2,1:T(8,128)(2,1)}, s32[]{:T(128)}) %tuple.131), condition=%wide.region_1.2_spmd, body=%wide.region_0.1_spmd.sunk | while | flops 100501760 | bytes 596805 | solution.py:25
  42.2 20.9 %while.76 = (s32[]{:T(128)}, bf16[6,128,256]{1,2,0:T(8,128)(2,1)}, bf16[6,128,256]{1,2,0:T(8,128)(2,1)S(1)}, bf16[6,39,256]{2,1,0:T(8,128)(2,1)S(1)}, bf16[128,128,39]{1,0,2:T(8,128)(2,1)}, /*index=5*/s32[]{:T(128)}) while((s32[]{:T(128)}, bf16[6,128,256]{1,2,0:T(8,128)(2,1)}, bf16[6,128,256]{1,2,0:T(8,128)(2,1)S(1)}, ...), condition=%wide.region_5.6_spmd, body=%wide.region_4.5_spmd.sunk | while | flops 329787136 | bytes 1771597 | solution.py:25
  42.2 3.5 fusion.114
  45.7 3.5 fusion.114
  49.2 3.5 fusion.114
  52.7 3.5 fusion.114
  65.0 25.9 %while.77 = (s32[]{:T(128)}, bf16[6,128,256]{1,2,0:T(8,128)(2,1)}, bf16[6,128,256]{1,2,0:T(8,128)(2,1)}, bf16[6,39,256]{2,1,0:T(8,128)(2,1)S(1)}, bf16[128,128,39]{1,0,2:T(8,128)(2,1)}, /*index=5*/s32[]{:T(128)}) while((s32[]{:T(128)}, bf16[6,128,256]{1,2,0:T(8,128)(2,1)}, bf16[6,128,256]{1,2,0:T(8,128)(2,1)}, ...), condition=%wide.region_9.10_spmd, body=%wide.region_8.9_spmd.sunk | while | flops 329787136 | bytes 1771597 | solution.py:25
  65.9 3.5 fusion.116
  83.2 3.5 fusion.116
  92.0 3.7 all-reduce
  99.4 60.1 %while.78 = (s32[]{:T(128)}, f32[128,128,39]{1,0,2:T(8,128)}, f32[6,128,256]{1,2,0:T(8,128)}, f32[6,39,256]{2,1,0:T(8,128)}, bf16[6,128,256]{1,2,0:T(8,128)(2,1)...) while((s32[]{:T(128)}, f32[128,128,39]{1,0,2:T(8,128)}, ...), condition=%wide.region_15.16_spmd.clone, body=%wide.region_12.15_spmd.clone.sunk | while | flops 663257088 | bytes 13271699 | solution.py:44
  109.7 4.3 %select_add_fusion.4 = f32[128,128,39]{1,0,2:T(8,128)} fusion(f32[128,128,39]{1,0,2:T(8,128)} %get-tuple-element.797, f32[39,256]{1,0:T(8,128)S(1)} %bitcast_convert_fusion.25, f32[128,256]{1,0:T(8,128)S(1)} %bitcast_convert_fusion.26, pred[]{:T(512)S(6)} %compare.9, bf16[6,128,256]{1,2,0:T(8,128)(2,1)} %get-tuple-element.810, s32[]{:T(128)} %get-tuple-element.796), kind=kOutput, calls=%fused_computation.34.clone.1 | convolution fusion | flops 330989568 | bytes 5348865 | tf_op jit(solution)/shard_map/while/body/eval_jaxpr/ol,cfl->ocf/dot_general | solution.py:33
  119.8 4.3 %select_add_fusion.4 = f32[128,128,39]{1,0,2:T(8,128)} fusion(f32[128,128,39]{1,0,2:T(8,128)} %get-tuple-element.797, f32[39,256]{1,0:T(8,128)S(1)} %bitcast_convert_fusion.25, f32[128,256]{1,0:T(8,128)S(1)} %bitcast_convert_fusion.26, pred[]{:T(512)S(6)} %compare.9, bf16[6,128,256]{1,2,0:T(8,128)(2,1)} %get-tuple-element.810, s32[]{:T(128)} %get-tuple-element.796), kind=kOutput, calls=%fused_computation.34.clone.1 | convolution fusion | flops 330989568 | bytes 5348865 | tf_op jit(solution)/shard_map/while/body/eval_jaxpr/ol,cfl->ocf/dot_general | solution.py:33
  130.0 4.3 %select_add_fusion.4 = f32[128,128,39]{1,0,2:T(8,128)} fusion(f32[128,128,39]{1,0,2:T(8,128)} %get-tuple-element.797, f32[39,256]{1,0:T(8,128)S(1)} %bitcast_convert_fusion.25, f32[128,256]{1,0:T(8,128)S(1)} %bitcast_convert_fusion.26, pred[]{:T(512)S(6)} %compare.9, bf16[6,128,256]{1,2,0:T(8,128)(2,1)} %get-tuple-element.810, s32[]{:T(128)} %get-tuple-element.796), kind=kOutput, calls=%fused_computation.34.clone.1 | convolution fusion | flops 330989568 | bytes 5348865 | tf_op jit(solution)/shard_map/while/body/eval_jaxpr/ol,cfl->ocf/dot_general | solution.py:33
  140.2 4.3 %select_add_fusion.4 = f32[128,128,39]{1,0,2:T(8,128)} fusion(f32[128,128,39]{1,0,2:T(8,128)} %get-tuple-element.797, f32[39,256]{1,0:T(8,128)S(1)} %bitcast_convert_fusion.25, f32[128,256]{1,0:T(8,128)S(1)} %bitcast_convert_fusion.26, pred[]{:T(512)S(6)} %compare.9, bf16[6,128,256]{1,2,0:T(8,128)(2,1)} %get-tuple-element.810, s32[]{:T(128)} %get-tuple-element.796), kind=kOutput, calls=%fused_computation.34.clone.1 | convolution fusion | flops 330989568 | bytes 5348865 | tf_op jit(solution)/shard_map/while/body/eval_jaxpr/ol,cfl->ocf/dot_general | solution.py:33
  150.3 4.3 %select_add_fusion.4 = f32[128,128,39]{1,0,2:T(8,128)} fusion(f32[128,128,39]{1,0,2:T(8,128)} %get-tuple-element.797, f32[39,256]{1,0:T(8,128)S(1)} %bitcast_convert_fusion.25, f32[128,256]{1,0:T(8,128)S(1)} %bitcast_convert_fusion.26, pred[]{:T(512)S(6)} %compare.9, bf16[6,128,256]{1,2,0:T(8,128)(2,1)} %get-tuple-element.810, s32[]{:T(128)} %get-tuple-element.796), kind=kOutput, calls=%fused_computation.34.clone.1 | convolution fusion | flops 330989568 | bytes 5348865 | tf_op jit(solution)/shard_map/while/body/eval_jaxpr/ol,cfl->ocf/dot_general | solution.py:33
  163.1 46.5 %while.79 = (s32[]{:T(128)}, f32[128,128,39]{1,0,2:T(8,128)S(1)}, f32[6,128,256]{1,2,0:T(8,128)}, f32[6,39,256]{2,1,0:T(8,128)}, bf16[6,128,256]{1,2,0:T(8,128)(...) while((s32[]{:T(128)}, f32[128,128,39]{1,0,2:T(8,128)S(1)}, ...), condition=%wide.region_19.20_spmd.clone, body=%wide.region_16.19_spmd.clone.sunk | while | flops 663257088 | bytes 13271699 | solution.py:44
  212.3 27.8 %while.80 = (s32[]{:T(128)}, f32[128,39,39]{0,2,1:T(8,128)}, f32[6,39,256]{2,1,0:T(8,128)S(1)}, f32[6,39,256]{2,1,0:T(8,128)}, bf16[6,128,256]{1,2,0:T(8,128)(2,...) while((s32[]{:T(128)}, f32[128,39,39]{0,2,1:T(8,128)}, ...), condition=%wide.region_23.24_spmd.clone, body=%wide.region_20.23_spmd.clone.sunk | while | flops 202076160 | bytes 2577003 | solution.py:44
  259.5 5.1 %all-to-all-start.1 = ((bf16[4,2,7680]{2,1,0:T(2,128)(2,1)}), bf16[4,2,7680]{2,1,0:T(2,128)(2,1)S(1)}, u32[]{:S(2)}, u32[]{:S(2)}) async-start(bf16[4,2,7680]{2,1,0:T(2,128)(2,1)} %reshape.220), calls=%async_computation.1 | async-start | bytes 245760 | tf_op jit(solution)/shard_map/all_to_all | solution.py:131
  264.6 6.6 %reduce-scatter.10.cloned.1.call-done = bf16[32,1521]{1,0:T(8,128)(2,1)} async-done(((bf16[128,1521]{1,0:T(8,128)(2,1)}), bf16[32,1521]{1,0:T(8,128)(2,1)}) %reduce-scatter.10.cloned.1.call-update) | async-done | bytes 97360
  273.1 30.4 %reduce-scatter.12.cloned.1.call-done = bf16[32,4992]{1,0:T(8,128)(2,1)} async-done(((bf16[128,4992]{1,0:T(8,128)(2,1)}), bf16[32,4992]{1,0:T(8,128)(2,1)}) %reduce-scatter.12.cloned.1.call-update) | async-done | bytes 319504
  305.7 30.0 %reduce-scatter.14.cloned.1.call-done = bf16[32,4992]{1,0:T(8,128)(2,1)} async-done(((bf16[128,4992]{1,0:T(8,128)(2,1)}), bf16[32,4992]{1,0:T(8,128)(2,1)}) %reduce-scatter.14.cloned.1.call-update) | async-done | bytes 319504
  340.9 71.5 %all-reduce.4.cloned.1.call-done = (bf16[32,1521]{0,1:T(8,128)(2,1)}, bf16[32,4992]{0,1:T(8,128)(2,1)}, bf16[32,4992]{0,1:T(8,128)(2,1)}) async-done(((bf16[32,1521]{0,1:T(8,128)(2,1)}, bf16[32,4992]{0,1:T(8,128)(2,1)}, bf16[32,4992]{0,1:T(8,128)(2,1)}), (bf16[32,1521]{0,1:T(8,128)(2,1)}, bf16[32,4992]{0,1:T(8,128)(2,1)}, bf16[32,4992]{0,1:T(8,128)(2,1)})) %all-reduce.4.cloned.1.call-update) | async-done | bytes 736336 | tf_op jit(solution)/shard_map/psum | solution.py:148
  (305 shorter events, 212.7 us)
Async XLA Ops:
  10.8 18.9 %all-to-all-start = ((bf16[4,2,7680]{2,1,0:T(2,128)(2,1)}), bf16[4,2,7680]{2,1,0:T(2,128)(2,1)S(1)}, u32[]{:S(2)}, u32[]{:S(2)}) async-start(bf16[4,2,7680]{2,1,0:T(2,128)(2,1)} %reshape.218), calls=%async_computation | async-start | bytes 245760 | tf_op jit(solution)/shard_map/all_to_all | solution.py:74
  17.1 254.1 %reduce-scatter.10.cloned.1.call-start = ((), (), s32[]{:S(2)}) async-start(), calls=%async_computation.5 | async-start | bytes 491520
  25.5 3.3 copy-start.10
  25.5 4.2 copy-start.12
  27.4 2.6 copy-start.15
  65.0 30.9 %copy-start.17 = (s32[24]{0:T(128)S(1)}, s32[24]{0:T(128)}, u32[]{:S(2)}) copy-start(s32[24]{0:T(128)} %param.23) | copy-start | bytes 292
  100.4 3.4 copy-start.3
  109.7 4.4 %copy-start.3 = (bf16[128,128,39]{0,1,2:T(8,128)(2,1)S(1)}, bf16[128,128,39]{0,1,2:T(8,128)(2,1)}, u32[]{:S(2)}) copy-start(bf16[128,128,39]{0,1,2:T(8,128)(2,1)} %get-tuple-element.813) | copy-start | bytes 3833860 | tf_op jit(solution)/shard_map/while
  119.8 4.4 %copy-start.3 = (bf16[128,128,39]{0,1,2:T(8,128)(2,1)S(1)}, bf16[128,128,39]{0,1,2:T(8,128)(2,1)}, u32[]{:S(2)}) copy-start(bf16[128,128,39]{0,1,2:T(8,128)(2,1)} %get-tuple-element.813) | copy-start | bytes 3833860 | tf_op jit(solution)/shard_map/while
  130.0 4.4 %copy-start.3 = (bf16[128,128,39]{0,1,2:T(8,128)(2,1)S(1)}, bf16[128,128,39]{0,1,2:T(8,128)(2,1)}, u32[]{:S(2)}) copy-start(bf16[128,128,39]{0,1,2:T(8,128)(2,1)} %get-tuple-element.813) | copy-start | bytes 3833860 | tf_op jit(solution)/shard_map/while
  140.2 4.4 %copy-start.3 = (bf16[128,128,39]{0,1,2:T(8,128)(2,1)S(1)}, bf16[128,128,39]{0,1,2:T(8,128)(2,1)}, u32[]{:S(2)}) copy-start(bf16[128,128,39]{0,1,2:T(8,128)(2,1)} %get-tuple-element.813) | copy-start | bytes 3833860 | tf_op jit(solution)/shard_map/while
  150.3 4.4 %copy-start.3 = (bf16[128,128,39]{0,1,2:T(8,128)(2,1)S(1)}, bf16[128,128,39]{0,1,2:T(8,128)(2,1)}, u32[]{:S(2)}) copy-start(bf16[128,128,39]{0,1,2:T(8,128)(2,1)} %get-tuple-element.813) | copy-start | bytes 3833860 | tf_op jit(solution)/shard_map/while
  163.3 2.8 copy-start.2
  171.0 2.8 copy-start.2
  178.8 2.8 copy-start.2
  186.6 2.8 copy-start.2
  194.3 2.8 copy-start.2
  202.0 2.8 copy-start.2
  244.9 58.6 %reduce-scatter.12.cloned.1.call-start = ((), (), s32[]{:S(2)}) async-start(), calls=%async_computation.6 | async-start | bytes 1597440
  249.6 2.7 copy-start.1
  252.2 83.5 %reduce-scatter.14.cloned.1.call-start = ((), (), s32[]{:S(2)}) async-start(), calls=%async_computation.7 | async-start | bytes 1597440
  259.5 78.5 %all-to-all-start.1 = ((bf16[4,2,7680]{2,1,0:T(2,128)(2,1)}), bf16[4,2,7680]{2,1,0:T(2,128)(2,1)S(1)}, u32[]{:S(2)}, u32[]{:S(2)}) async-start(bf16[4,2,7680]{2,1,0:T(2,128)(2,1)} %reshape.220), calls=%async_computation.1 | async-start | bytes 245760 | tf_op jit(solution)/shard_map/all_to_all | solution.py:131
  264.6 147.7 %all-reduce.4.cloned.1.call-start = ((), (), s32[]{:S(2)}) async-start(), calls=%async_computation.8 | async-start | bytes 5894144 | tf_op jit(solution)/shard_map/psum | solution.py:148
  412.3 4.1 copy-start.11
  (10 other events, 16.5 us)
Sparse Core Ops, SparseCore 0:
  245.0 26.1 reduce-scatter.9
  274.1 29.2 reduce-scatter.11
  306.4 29.2 reduce-scatter.13
  338.8 73.5 all-reduce.3
where the time goes:
time: 427 us; the launch traced here: 424 us
  matrix products  151 us (35%)
  waiting for transfers between devices  139 us (33%)
  local copies, waits for them, and re-layouts  86.5 us (20%)
  other arithmetic  17.9 us (4%)
  between operations  14.1 us (3%)
  starting transfers between devices  11.5 us (3%)
    psum x1, waiting for transfers between devices, local(): lax.psum(shares[0].astype(jnp.bfloat16), ('samp', 'col'))  71.5 us
    unnamed x7, waiting for transfers between devices  67.1 us
    dot_general x18, matrix products, accumulate(): jnp.einsum('ol,cfl->ocf', cotangent_part, outer_products, preferred_eleme...  56.2 us
    dot_general x18, matrix products, one_block(): jnp.einsum('ocf,cfl->ol', filter_cube, outer_products, preferred_element_...  50.2 us
    dot_general x18, matrix products, accumulate(): jnp.einsum('ocf,ol->cfl', filter_cube, cotangent_part, preferred_element_...  39.7 us
    dynamic_update_slice x42, local copies, waits for them, and re-layouts, backward_layer(): lax.scan(accumulate, starting, (cotangent, previous, anchor))  31.1 us
    unnamed x49, local copies, waits for them, and re-layouts  27 us
  transfers between devices with their start and end apart: 6, of which 4 were waited for; matrix products, arithmetic and copies ran while one was open for 8% of the time, Pallas kernels for 0%

commit v1 on v0

--- a/solution.py
+++ b/solution.py
@@ -145,7 +145,9 @@
         ).astype(jnp.float32),
     )
     summed = (
-        lax.psum(shares[0].astype(jnp.bfloat16), ("samp", "col")).astype(jnp.float32),
+        jnp.sum(lax.all_gather(shares[0].astype(jnp.bfloat16), ("samp", "col")), axis=0).astype(
+            jnp.float32
+        ),
         lax.psum(shares[1].astype(jnp.bfloat16), ("samp", "col")).astype(jnp.float32),
         lax.psum(shares[2].astype(jnp.bfloat16), ("samp", "col")).astype(jnp.float32),
     )

time: 427 us -> 396 us (0.927)
  blocking collectives: 3.68 us -> 33.4 us
  waiting for transfers between devices: 139 us -> 111 us
  matrix products: 151 us -> 132 us
  local copies, waits for them, and re-layouts: 86.5 us -> 80 us
  starting transfers between devices: 11.5 us -> 6.47 us
    unnamed x7 -> x6, waiting for transfers between devices: 67.1 us -> 31.3 us
    reduce_scatter x0 -> x1, waiting for transfers between devices: none -> 25.8 us  [local(): lax.psum_scatter(grad_one.astype(jnp.bfloat16), 'dp', scatter_dimension=0...]
    all_gather x0 -> x1, blocking collectives: none -> 18.6 us  [local(): lax.all_gather(shares[0].astype(jnp.bfloat16), ('samp', 'col'))]
    psum x1, waiting for transfers between devices: 71.5 us -> 53.5 us  [local(): lax.psum(shares[1].astype(jnp.bfloat16), ('samp', 'col'))]
    dot_general x18, matrix products: 56.2 us -> 44.2 us  [accumulate(): jnp.einsum('ol,cfl->ocf', cotangent_part, outer_products, preferred_eleme...]
    all_to_all x0 -> x1, blocking collectives: none -> 11.1 us  [local(): lax.all_to_all(slot_grads, 'samp', split_axis=1, concat_axis=0, tiled=True)]
    dot_general x18, matrix products: 39.7 us -> 33.5 us  [accumulate(): jnp.einsum('ocf,ol->cfl', filter_cube, cotangent_part, preferred_element_...]
    all_to_all x1 -> x0, starting transfers between devices: 5.09 us -> none  [local(): lax.all_to_all(slot_grads, 'samp', split_axis=1, concat_axis=0, tiled=True)]
  transfers between devices with their start and end apart: 6 -> 5, of which waited for: 4 -> 4; matrix products, arithmetic and copies ran while one was open for 8% -> 10% of each run, Pallas kernels for 0% -> 0%
where the time goes in v1:
time: 396 us; the launch traced here: 393 us
  matrix products  132 us (33%)
  waiting for transfers between devices  111 us (28%)
  local copies, waits for them, and re-layouts  80 us (20%)
  blocking collectives  33.4 us (8%)
  other arithmetic  15 us (4%)
  between operations  14.1 us (4%)
  starting transfers between devices  6.47 us (2%)
    psum x1, waiting for transfers between devices, local(): lax.psum(shares[1].astype(jnp.bfloat16), ('samp', 'col'))  53.5 us
    dot_general x18, matrix products, one_block(): jnp.einsum('ocf,cfl->ol', filter_cube, outer_products, preferred_element_...  50.1 us
    dot_general x18, matrix products, accumulate(): jnp.einsum('ol,cfl->ocf', cotangent_part, outer_products, preferred_eleme...  44.2 us
    dot_general x18, matrix products, accumulate(): jnp.einsum('ocf,ol->cfl', filter_cube, cotangent_part, preferred_element_...  33.5 us
    unnamed x6, waiting for transfers between devices  31.3 us
    dynamic_update_slice x42, local copies, waits for them, and re-layouts, backward_layer(): lax.scan(accumulate, starting, (cotangent, previous, anchor))  27.5 us
    reduce_scatter x1, waiting for transfers between devices, local(): lax.psum_scatter(grad_one.astype(jnp.bfloat16), 'dp', scatter_dimension=0...  25.8 us
    unnamed x49, local copies, waits for them, and re-layouts  23.1 us
  transfers between devices with their start and end apart: 5, of which 4 were waited for; matrix products, arithmetic and copies ran while one was open for 10% of the time, Pallas kernels for 0%

profile of v1, /device:TPU:0, one launch (start us, length us, event | category | flops | bytes accessed | tf_op | source)
XLA Modules:
  0.0 393.2 jit_solution(18208288964585382873)
XLA Ops:
  10.8 6.3 %all-to-all-start = ((bf16[4,2,7680]{2,1,0:T(2,128)(2,1)}), bf16[4,2,7680]{2,1,0:T(2,128)(2,1)S(1)}, u32[]{:S(2)}, u32[]{:S(2)}) async-start(bf16[4,2,7680]{2,1,0:T(2,128)(2,1)} %reshape.219), calls=%async_computation | async-start | bytes 245760 | tf_op jit(solution)/shard_map/all_to_all | solution.py:74
  34.0 9.0 %while.75 = (s32[]{:T(128)}, bf16[6,128,256]{1,2,0:T(8,128)(2,1)S(1)}, bf16[6,39,256]{2,1,0:T(8,128)(2,1)S(1)}, bf16[128,39,39]{0,2,1:T(8,128)(2,1)}, s32[]{:T(128)}) while((s32[]{:T(128)}, bf16[6,128,256]{1,2,0:T(8,128)(2,1)S(1)}, bf16[6,39,256]{2,1,0:T(8,128)(2,1)S(1)}, bf16[128,39,39]{0,2,1:T(8,128)(2,1)}, s32[]{:T(128)}) %tuple.137), condition=%wide.region_1.2_spmd, body=%wide.region_0.1_spmd.sunk | while | flops 100501760 | bytes 596805 | solution.py:25
  43.8 20.9 %while.76 = (s32[]{:T(128)}, bf16[6,128,256]{1,2,0:T(8,128)(2,1)}, bf16[6,128,256]{1,2,0:T(8,128)(2,1)S(1)}, bf16[6,39,256]{2,1,0:T(8,128)(2,1)S(1)}, bf16[128,128,39]{1,0,2:T(8,128)(2,1)}, /*index=5*/s32[]{:T(128)}) while((s32[]{:T(128)}, bf16[6,128,256]{1,2,0:T(8,128)(2,1)}, bf16[6,128,256]{1,2,0:T(8,128)(2,1)S(1)}, ...), condition=%wide.region_5.6_spmd, body=%wide.region_4.5_spmd.sunk | while | flops 329787136 | bytes 1771597 | solution.py:25
  43.9 3.4 fusion.114
  47.3 3.4 fusion.114
  50.8 3.4 fusion.114
  57.8 3.4 fusion.114
  66.6 25.9 %while.77 = (s32[]{:T(128)}, bf16[6,128,256]{1,2,0:T(8,128)(2,1)}, bf16[6,128,256]{1,2,0:T(8,128)(2,1)}, bf16[6,39,256]{2,1,0:T(8,128)(2,1)S(1)}, bf16[128,128,39]{1,0,2:T(8,128)(2,1)}, /*index=5*/s32[]{:T(128)}) while((s32[]{:T(128)}, bf16[6,128,256]{1,2,0:T(8,128)(2,1)}, bf16[6,128,256]{1,2,0:T(8,128)(2,1)}, ...), condition=%wide.region_9.10_spmd, body=%wide.region_8.9_spmd.sunk | while | flops 329787136 | bytes 1771597 | solution.py:25
  71.8 3.5 fusion.116
  89.1 3.4 fusion.116
  93.6 3.7 all-reduce
  100.9 60.1 %while.78 = (s32[]{:T(128)}, f32[128,128,39]{1,0,2:T(8,128)}, f32[6,128,256]{1,2,0:T(8,128)}, f32[6,39,256]{2,1,0:T(8,128)}, bf16[6,128,256]{1,2,0:T(8,128)(2,1)...) while((s32[]{:T(128)}, f32[128,128,39]{1,0,2:T(8,128)}, ...), condition=%wide.region_15.16_spmd.clone, body=%wide.region_12.15_spmd.clone.sunk | while | flops 663257088 | bytes 13271699 | solution.py:44
  111.2 4.3 %select_add_fusion.4 = f32[128,128,39]{1,0,2:T(8,128)} fusion(f32[128,128,39]{1,0,2:T(8,128)} %get-tuple-element.833, f32[39,256]{1,0:T(8,128)S(1)} %bitcast_convert_fusion.25, f32[128,256]{1,0:T(8,128)S(1)} %bitcast_convert_fusion.26, pred[]{:T(512)S(6)} %compare.9, bf16[6,128,256]{1,2,0:T(8,128)(2,1)} %get-tuple-element.846, s32[]{:T(128)} %get-tuple-element.832), kind=kOutput, calls=%fused_computation.34.clone.1 | convolution fusion | flops 330989568 | bytes 5348865 | tf_op jit(solution)/shard_map/while/body/eval_jaxpr/ol,cfl->ocf/dot_general | solution.py:33
  121.4 4.3 %select_add_fusion.4 = f32[128,128,39]{1,0,2:T(8,128)} fusion(f32[128,128,39]{1,0,2:T(8,128)} %get-tuple-element.833, f32[39,256]{1,0:T(8,128)S(1)} %bitcast_convert_fusion.25, f32[128,256]{1,0:T(8,128)S(1)} %bitcast_convert_fusion.26, pred[]{:T(512)S(6)} %compare.9, bf16[6,128,256]{1,2,0:T(8,128)(2,1)} %get-tuple-element.846, s32[]{:T(128)} %get-tuple-element.832), kind=kOutput, calls=%fused_computation.34.clone.1 | convolution fusion | flops 330989568 | bytes 5348865 | tf_op jit(solution)/shard_map/while/body/eval_jaxpr/ol,cfl->ocf/dot_general | solution.py:33
  131.5 4.3 %select_add_fusion.4 = f32[128,128,39]{1,0,2:T(8,128)} fusion(f32[128,128,39]{1,0,2:T(8,128)} %get-tuple-element.833, f32[39,256]{1,0:T(8,128)S(1)} %bitcast_convert_fusion.25, f32[128,256]{1,0:T(8,128)S(1)} %bitcast_convert_fusion.26, pred[]{:T(512)S(6)} %compare.9, bf16[6,128,256]{1,2,0:T(8,128)(2,1)} %get-tuple-element.846, s32[]{:T(128)} %get-tuple-element.832), kind=kOutput, calls=%fused_computation.34.clone.1 | convolution fusion | flops 330989568 | bytes 5348865 | tf_op jit(solution)/shard_map/while/body/eval_jaxpr/ol,cfl->ocf/dot_general | solution.py:33
  141.7 4.3 %select_add_fusion.4 = f32[128,128,39]{1,0,2:T(8,128)} fusion(f32[128,128,39]{1,0,2:T(8,128)} %get-tuple-element.833, f32[39,256]{1,0:T(8,128)S(1)} %bitcast_convert_fusion.25, f32[128,256]{1,0:T(8,128)S(1)} %bitcast_convert_fusion.26, pred[]{:T(512)S(6)} %compare.9, bf16[6,128,256]{1,2,0:T(8,128)(2,1)} %get-tuple-element.846, s32[]{:T(128)} %get-tuple-element.832), kind=kOutput, calls=%fused_computation.34.clone.1 | convolution fusion | flops 330989568 | bytes 5348865 | tf_op jit(solution)/shard_map/while/body/eval_jaxpr/ol,cfl->ocf/dot_general | solution.py:33
  151.9 4.3 %select_add_fusion.4 = f32[128,128,39]{1,0,2:T(8,128)} fusion(f32[128,128,39]{1,0,2:T(8,128)} %get-tuple-element.833, f32[39,256]{1,0:T(8,128)S(1)} %bitcast_convert_fusion.25, f32[128,256]{1,0:T(8,128)S(1)} %bitcast_convert_fusion.26, pred[]{:T(512)S(6)} %compare.9, bf16[6,128,256]{1,2,0:T(8,128)(2,1)} %get-tuple-element.846, s32[]{:T(128)} %get-tuple-element.832), kind=kOutput, calls=%fused_computation.34.clone.1 | convolution fusion | flops 330989568 | bytes 5348865 | tf_op jit(solution)/shard_map/while/body/eval_jaxpr/ol,cfl->ocf/dot_general | solution.py:33
  164.6 46.6 %while.79 = (s32[]{:T(128)}, f32[128,128,39]{1,0,2:T(8,128)S(1)}, f32[6,128,256]{1,2,0:T(8,128)}, f32[6,39,256]{2,1,0:T(8,128)}, bf16[6,128,256]{1,2,0:T(8,128)(...) while((s32[]{:T(128)}, f32[128,128,39]{1,0,2:T(8,128)S(1)}, ...), condition=%wide.region_19.20_spmd.clone, body=%wide.region_16.19_spmd.clone.sunk | while | flops 663257088 | bytes 13271699 | solution.py:44
  226.1 6.3 %while.80 = (s32[]{:T(128)}, f32[128,39,39]{0,2,1:T(8,128)S(1)}, f32[6,39,256]{2,1,0:T(8,128)S(1)}, f32[6,39,256]{2,1,0:T(8,128)S(1)}, bf16[6,128,256]{1,2,0:T(8...) while((s32[]{:T(128)}, f32[128,39,39]{0,2,1:T(8,128)S(1)}, ...), condition=%wide.region_23.24_spmd.clone, body=%wide.region_20.23_spmd.clone.sunk | while | flops 202076160 | bytes 2575479 | solution.py:44
  234.4 11.1 %all_to_all.30 = bf16[4,2,7680]{2,1,0:T(2,128)(2,1)S(1)} all-to-all(bf16[4,2,7680]{2,1,0:T(2,128)(2,1)S(1)} %reshape.221), channel_id=1, replica_groups=mesh['dp'=4,'samp'=4,'col'=2] {'samp'}, dimensions={0} | all-to-all | bytes 245760 | tf_op jit(solution)/shard_map/all_to_all | solution.py:131
  251.7 30.0 %reduce-scatter.14.cloned.1.call-done = bf16[32,4992]{1,0:T(8,128)(2,1)} async-done(((bf16[128,4992]{1,0:T(8,128)(2,1)}), bf16[32,4992]{1,0:T(8,128)(2,1)}) %reduce-scatter.14.cloned.1.call-update) | async-done | bytes 319504
  284.0 25.8 %reduce-scatter.10.cloned.1.call-done = bf16[32,1521]{1,0:T(8,128)(2,1)} async-done(((bf16[128,1521]{1,0:T(8,128)(2,1)}), bf16[32,1521]{1,0:T(8,128)(2,1)}) %reduce-scatter.10.cloned.1.call-update) | async-done | bytes 97360 | tf_op jit(solution)/shard_map/reduce_scatter | solution.py:137
  309.8 18.6 %all-gather = bf16[256,1521]{1,0:T(8,128)(2,1)S(1)} all-gather(bf16[32,1521]{1,0:T(8,128)(2,1)} %reduce-scatter.10.cloned.1.call-done), channel_id=2, replica_groups=mesh['dp'=4,'samp'=4,'col'=2] {'samp','col'}, dimensions={0}, use_global_device_ids=true | all-gather | bytes 876096 | tf_op jit(solution)/shard_map/all_gather | solution.py:148
  329.2 53.5 %all-reduce.4.cloned.1.call-done = (bf16[32,4992]{0,1:T(8,128)(2,1)}, bf16[32,4992]{0,1:T(8,128)(2,1)}) async-done(((bf16[32,4992]{0,1:T(8,128)(2,1)}, bf16[32,4992]{0,1:T(8,128)(2,1)}), (bf16[32,4992]{0,1:T(8,128)(2,1)}, bf16[32,4992]{0,1:T(8,128)(2,1)})) %all-reduce.4.cloned.1.call-update) | async-done | bytes 638992 | tf_op jit(solution)/shard_map/psum | solution.py:151
  (307 shorter events, 186.4 us)
Async XLA Ops:
  8.1 9.0 %copy-start.4 = (bf16[128,4992]{1,0:T(8,128)(2,1)S(1)}, bf16[128,4992]{1,0:T(8,128)(2,1)}, u32[]{:S(2)}) copy-start(bf16[128,4992]{1,0:T(8,128)(2,1)} %param.27) | copy-start | bytes 3833860
  10.8 22.2 %all-to-all-start = ((bf16[4,2,7680]{2,1,0:T(2,128)(2,1)}), bf16[4,2,7680]{2,1,0:T(2,128)(2,1)S(1)}, u32[]{:S(2)}, u32[]{:S(2)}) async-start(bf16[4,2,7680]{2,1,0:T(2,128)(2,1)} %reshape.219), calls=%async_computation | async-start | bytes 245760 | tf_op jit(solution)/shard_map/all_to_all | solution.py:74
  17.1 232.3 %reduce-scatter.12.cloned.1.call-start = ((), (), s32[]{:S(2)}) async-start(), calls=%async_computation.6 | async-start | bytes 1597440
  28.8 3.3 copy-start.11
  28.8 4.2 %copy-start.13 = (bf16[3,128]{1,0:T(4,128)(2,1)S(1)}, bf16[3,128]{1,0:T(4,128)(2,1)}, u32[]{:S(2)}) copy-start(bf16[3,128]{1,0:T(4,128)(2,1)} %param.24) | copy-start | bytes 2308
  66.6 30.9 %copy-start.18 = (s32[24]{0:T(128)S(1)}, s32[24]{0:T(128)}, u32[]{:S(2)}) copy-start(s32[24]{0:T(128)} %param.23) | copy-start | bytes 292
  101.9 3.4 copy-start.6
  111.2 4.3 %copy-start.6 = (bf16[128,128,39]{0,1,2:T(8,128)(2,1)S(1)}, bf16[128,128,39]{0,1,2:T(8,128)(2,1)}, u32[]{:S(2)}) copy-start(bf16[128,128,39]{0,1,2:T(8,128)(2,1)} %get-tuple-element.849) | copy-start | bytes 3833860 | tf_op jit(solution)/shard_map/while
  121.3 4.3 %copy-start.6 = (bf16[128,128,39]{0,1,2:T(8,128)(2,1)S(1)}, bf16[128,128,39]{0,1,2:T(8,128)(2,1)}, u32[]{:S(2)}) copy-start(bf16[128,128,39]{0,1,2:T(8,128)(2,1)} %get-tuple-element.849) | copy-start | bytes 3833860 | tf_op jit(solution)/shard_map/while
  131.5 4.3 %copy-start.6 = (bf16[128,128,39]{0,1,2:T(8,128)(2,1)S(1)}, bf16[128,128,39]{0,1,2:T(8,128)(2,1)}, u32[]{:S(2)}) copy-start(bf16[128,128,39]{0,1,2:T(8,128)(2,1)} %get-tuple-element.849) | copy-start | bytes 3833860 | tf_op jit(solution)/shard_map/while
  141.7 4.3 %copy-start.6 = (bf16[128,128,39]{0,1,2:T(8,128)(2,1)S(1)}, bf16[128,128,39]{0,1,2:T(8,128)(2,1)}, u32[]{:S(2)}) copy-start(bf16[128,128,39]{0,1,2:T(8,128)(2,1)} %get-tuple-element.849) | copy-start | bytes 3833860 | tf_op jit(solution)/shard_map/while
  151.9 4.3 %copy-start.6 = (bf16[128,128,39]{0,1,2:T(8,128)(2,1)S(1)}, bf16[128,128,39]{0,1,2:T(8,128)(2,1)}, u32[]{:S(2)}) copy-start(bf16[128,128,39]{0,1,2:T(8,128)(2,1)} %get-tuple-element.849) | copy-start | bytes 3833860 | tf_op jit(solution)/shard_map/while
  164.8 2.8 copy-start.5
  172.6 2.8 copy-start.5
  180.3 2.8 copy-start.5
  188.1 2.8 copy-start.5
  195.9 2.8 copy-start.5
  203.6 2.8 copy-start.5
  218.6 63.1 %reduce-scatter.14.cloned.1.call-start = ((), (), s32[]{:S(2)}) async-start(), calls=%async_computation.7 | async-start | bytes 1597440
  223.3 2.8 copy-start.2
  223.3 2.8 copy-start.10
  225.9 83.9 %reduce-scatter.10.cloned.1.call-start = ((), (), s32[]{:S(2)}) async-start(), calls=%async_computation.5 | async-start | bytes 491520 | tf_op jit(solution)/shard_map/reduce_scatter | solution.py:137
  233.7 12.3 %copy-start.15 = (s32[1920]{0:T(1024)S(1)}, s32[1920]{0:T(1024)}, u32[]{:S(2)}) copy-start(s32[1920]{0:T(1024)} %copy-done.14) | copy-start | bytes 23044
  233.7 149.0 %all-reduce.4.cloned.1.call-start = ((), (), s32[]{:S(2)}) async-start(), calls=%async_computation.8 | async-start | bytes 5111808 | tf_op jit(solution)/shard_map/psum | solution.py:151
  (10 other events, 19.4 us)
Sparse Core Ops, SparseCore 0:
  218.7 30.7 reduce-scatter.11
  252.4 29.2 reduce-scatter.13
  285.0 24.7 reduce-scatter.9
  312.1 70.5 all-reduce.3
